TPU v7x, 32 devices: a whole 2x2x4 slice. The times are simulated.
32 devices in a mesh: tower: 2 (over core), tp: 4 (over z), grp: 4 (over y, x).
Axes of the slice: x: 2, y: 2, z: 4, core: 2. Of those that a mesh axis runs over, the one named last changes fastest.
Arguments:
- tokens: bfloat16 [3072, 8192], P('grp', 'tp'), may hold values from -700 to 700
- modality: int32 [3072], P('grp'), may hold values from 0 to 1, as said below
- doc_ids: int32 [3072], P('grp'), may hold values from 0 to 15, as said below
- owner_ids: int32 [3072], P('grp'), may hold values from 0 to 3, as said below
- norm_gain: float32 [2, 8192], P('tower'), may hold values from 0.5 to 1.5
- query_weight: bfloat16 [2, 8192, 4096], P('tower', 'grp', 'tp'), may hold values from -0.125 to 0.125
- pair_weight: bfloat16 [2, 8192, 1024], P('tower', 'grp'), may hold values from -0.125 to 0.125
Outputs:
- attended: bfloat16 [2, 3072, 4096], P('tower', 'grp', 'tp')
Inputs may be any that keep to these rules, and one draw needn't show every extreme that they name: Every group of 768 tokens holds exactly 384 tokens of each modality. `owner_ids`: within every group each owner is named by exactly 192 tokens, and by at most 192 tokens of one modality. `doc_ids`: all tokens of one document have the same owner.
All inputs are finite; a program needn't handle non-finite values.
Results may differ from a plain program's by a relative error of at most 0.0084.
Values may be sent and summed in bfloat16 or wider, within the bound.
A program may use at most 128 MiB of HBM per device.

v0:
```python
import math

import jax
import jax.numpy as jnp
from jax import lax
from jax.sharding import PartitionSpec as P

HD = 128


EPS = 1e-05
MASKED = -1e30


def from_partner(value, axis, stride):
    mask = 2**stride
    pairs = [(source, source ^ mask) for source in range(lax.axis_size(axis))]
    return lax.ppermute(value, axis, pairs)


def local(tokens, modality, doc_ids, owner_ids, norm_gain, query_weight, pair_weight):
    groups = lax.axis_size("grp")
    tp_count = lax.axis_size("tp")
    tower_index = lax.axis_index("tower")
    group_index = lax.axis_index("grp")
    tp_rank = lax.axis_index("tp")
    tok_count = tokens.shape[0]
    half_rows = tok_count // 2
    slot_count = tok_count // groups
    total_slots = groups * slot_count
    head_cols = query_weight.shape[2]
    pair_cols = pair_weight.shape[2]
    pair_heads = pair_cols // (2 * HD)
    own_head = tp_rank // (tp_count // pair_heads)
    in_tower = modality == tower_index
    positions = jnp.arange(tok_count, dtype=jnp.int32)
    packed_rank = jnp.cumsum(in_tower.astype(jnp.int32)) - 1
    row_index = (
        jnp.zeros((half_rows,), jnp.int32)
        .at[jnp.where(in_tower, packed_rank, half_rows)]
        .set(positions, mode="drop")
    )
    chosen = tokens[row_index]
    features = lax.all_gather(chosen, "tp", axis=1, tiled=True)
    values = features.astype(jnp.float32)
    inverse_rms = lax.rsqrt(jnp.mean(values * values, axis=1, keepdims=True) + EPS)
    normed = (values * inverse_rms * norm_gain[0][None, :]).astype(jnp.bfloat16)
    query_local = query_weight[0]
    pair_local = pair_weight[0]
    pair_part = lax.dynamic_slice_in_dim(pair_local, own_head * 2 * HD, 2 * HD, 1)
    pieces = (
        lax.all_gather(query_local, "grp", axis=0, tiled=True),
        lax.all_gather(pair_part, "grp", axis=0, tiled=True),
    )
    totals = tuple(
        (jnp.dot(normed, weight_rows, preferred_element_type=jnp.float32) for weight_rows in pieces)
    )
    query_rows = totals[0].astype(jnp.bfloat16)
    pair_rows = totals[1].astype(jnp.bfloat16)
    owner_onehot = (
        (owner_ids[:, None] == jnp.arange(groups, dtype=jnp.int32)[None, :]) & in_tower[:, None]
    ).astype(jnp.int32)
    slot_rank = jnp.sum((jnp.cumsum(owner_onehot, axis=0) - 1) * owner_onehot, axis=1)
    destination = jnp.where(in_tower, owner_ids * slot_count + slot_rank, total_slots)
    source_row = (
        jnp.full((total_slots,), half_rows, jnp.int32).at[destination].set(packed_rank, mode="drop")
    )
    filled = source_row < half_rows
    safe_row = jnp.minimum(source_row, half_rows - 1)
    zero_value = jnp.zeros((), jnp.bfloat16)
    query_send = jnp.where(filled[:, None], query_rows[safe_row], zero_value)
    pair_send = jnp.where(filled[:, None], pair_rows[safe_row], zero_value)
    token_row = row_index[safe_row]
    doc_send = jnp.where(filled, doc_ids[token_row], -1)
    place_send = jnp.where(filled, group_index * tok_count + token_row, -1)
    query_in, pair_in, doc_in, place_in = (
        lax.all_to_all(query_send, "grp", split_axis=0, concat_axis=0, tiled=True),
        lax.all_to_all(pair_send, "grp", split_axis=0, concat_axis=0, tiled=True),
        lax.all_to_all(doc_send, "grp", split_axis=0, concat_axis=0, tiled=True),
        lax.all_to_all(place_send, "grp", split_axis=0, concat_axis=0, tiled=True),
    )
    pair_other, doc_other, place_other = from_partner((pair_in, doc_in, place_in), "tower", 0)
    key_rows = jnp.concatenate([pair_in[:, :HD], pair_other[:, :HD]], axis=0)
    value_rows = jnp.concatenate([pair_in[:, HD:], pair_other[:, HD:]], axis=0)
    doc_keys = jnp.concatenate([doc_in, doc_other], axis=0)
    place_keys = jnp.concatenate([place_in, place_other], axis=0)
    is_image = tower_index == 1
    image_keys = jnp.concatenate(
        [jnp.full((total_slots,), is_image), jnp.full((total_slots,), jnp.logical_not(is_image))],
        axis=0,
    )
    heads_here = head_cols // HD
    queries = query_in.reshape(total_slots, heads_here, HD)
    scores = jnp.einsum("qhd,kd->hqk", queries, key_rows, preferred_element_type=jnp.float32) * (
        1.0 / math.sqrt(HD)
    )
    allowed = (doc_in[:, None] == doc_keys[None, :]) & (
        (place_keys[None, :] <= place_in[:, None]) | is_image & image_keys[None, :]
    )
    scores = jnp.where(allowed[None], scores, MASKED)
    row_max = jnp.max(scores, axis=2, keepdims=True)
    powered = jnp.exp(scores - row_max)
    weights = (powered / jnp.sum(powered, axis=2, keepdims=True)).astype(jnp.bfloat16)
    mixed_rows = jnp.einsum("hqk,kd->qhd", weights, value_rows, preferred_element_type=jnp.float32)
    mixed_rows = mixed_rows.astype(jnp.bfloat16).reshape(total_slots, head_cols)
    returned = lax.all_to_all(mixed_rows, "grp", split_axis=0, concat_axis=0, tiled=True)
    safe_dest = jnp.minimum(destination, total_slots - 1)
    result = jnp.where(in_tower[:, None], returned[safe_dest], zero_value)
    return result[None]


def solution(mesh):
    in_specs = (
        P("grp", "tp"),
        P("grp"),
        P("grp"),
        P("grp"),
        P("tower", None),
        P("tower", "grp", "tp"),
        P("tower", "grp", None),
    )
    out_specs = P("tower", "grp", "tp")
    return jax.shard_map(local, mesh=mesh, in_specs=in_specs, out_specs=out_specs, check_vma=False)
```

profile of v0, /device:TPU:0, one launch (start us, length us, event | category | flops | bytes accessed | tf_op | source)
XLA Modules:
  0.0 466.9 jit_solution(12720124636309830133)
XLA Ops:
  6.5 0.8 bitcast_convert_fusion
  7.4 0.3 reduce-window.19
  7.7 0.1 slice.27
  7.8 0.1 slice_reduce_fusion.1
  7.9 0.7 fusion.39
  8.6 1.1 reduce-window.15
  9.7 0.2 slice_reduce_fusion
  9.9 0.2 reduce-window.16
  10.1 0.1 add_bitcast_fusion
  10.2 0.7 fusion.41
  10.9 0.8 compare_select_fusion.1
  11.7 3.4 scatter_custom_fusion.1
  15.1 3.1 gather_fusion
  18.2 0.0 all-gather.7.cloned.1.call-update
  18.2 0.0 all-gather.9.cloned.1.call-start
  18.3 2.3 constant_dynamic-slice_fusion
  20.5 0.0 all-gather.9.cloned.1.call-update
  20.6 0.0 copy-start.2
  20.6 0.0 all-gather.11.cloned.1.call-start
  20.6 0.7 all-gather.11.cloned.1.call-update
  21.3 3.4 scatter_custom_fusion
  24.7 5.0 %gather_fusion.2 = s32[768]{0:T(1024)S(1)} fusion(s32[384]{0:T(512)S(1)} %scatter_custom_fusion.1, s32[1024]{0:T(1024)S(1)} %pad_clamp_fusion.2), kind=kCustom, calls=%fused_computation.2 | custom fusion | bytes 9216 | tf_op jit(solution)/shard_map/gather | solution.py:73
  29.8 3.2 gather_fusion.3
  33.0 0.0 copy-start.4
  33.0 0.7 all_to_all.44
  33.7 5.2 %all-to-all-start.2 = ((s32[4,192,1]{1,2,0:T(1,128)}), s32[4,192,1]{1,2,0:T(1,128)S(1)}, u32[]{:S(2)}, u32[]{:S(2)}) async-start(s32[4,192,1]{1,2,0:T(1,128)} %all_to_all.44), calls=%async_computation.2 | async-start | bytes 8192 | tf_op jit(solution)/shard_map/all_to_all | solution.py:80
  38.9 0.7 all_to_all.43
  39.5 3.9 all-to-all-done.2
  43.4 3.2 all-to-all-start.1
  46.6 0.1 broadcast_in_dim.96
  46.8 0.1 all_to_all.38
  46.8 4.4 all-to-all-done.1
  51.3 0.1 eq.60
  51.4 0.0 collective-permute-start.1
  51.4 0.5 collective-permute-start.2
  51.9 84.5 %all-gather.7.cloned.1.call-done = bf16[384,8192]{1,0:T(8,128)(2,1)} async-done(((bf16[384,2048]{1,0:T(8,128)(2,1)}), bf16[384,8192]{1,0:T(8,128)(2,1)}) %all-gather.7.cloned.1.call-update) | async-done | bytes 6291472 | tf_op jit(solution)/shard_map/all_gather | solution.py:44
  136.4 4.1 fusion.8
  140.5 48.5 %all-gather.9.cloned.1.call-done = bf16[1,8192,256]{2,1,0:T(8,128)(2,1)} async-done(((bf16[1,2048,256]{2,1,0:T(8,128)(2,1)}), bf16[1,8192,256]{2,1,0:T(8,128)(2,1)}) %all-gather.9.cloned.1.call-update) | async-done | bytes 4194320 | tf_op jit(solution)/shard_map/all_gather | solution.py:53
  189.0 5.9 %fusion.31 = bf16[384,256]{1,0:T(8,128)(2,1)S(1)} fusion(bf16[1,8192,256]{2,1,0:T(8,128)(2,1)} %all-gather.9.cloned.1.call-done, bf16[384,8192]{1,0:T(8,128)(2,1)} %all-gather.7.cloned.1.call-done, f32[8192]{0:T(1024)S(1)} %bitcast.78, f32[384]{0:T(512)S(1)} %add_rsqrt_fusion), kind=kOutput, calls=%fused_computation.36 | convolution fusion | flops 1623293952 | bytes 10716672 | tf_op jit(solution)/shard_map/dot_general | solution.py:56
  194.9 2.7 gather_fusion.1
  197.6 0.9 broadcast_select_fusion.1
  198.5 3.7 all-to-all-start
  202.2 149.2 %all-gather.11.cloned.1.call-done = bf16[1,8192,1024]{2,1,0:T(8,128)(2,1)} async-done(((bf16[1,2048,1024]{2,1,0:T(8,128)(2,1)}), bf16[1,8192,1024]{2,1,0:T(8,128)(2,1)}) %all-gather.11.cloned.1.call-update) | async-done | bytes 16777232 | tf_op jit(solution)/shard_map/all_gather | solution.py:52
  351.4 12.2 %fusion.19 = bf16[384,1024]{1,0:T(8,128)(2,1)S(1)} fusion(bf16[1,8192,1024]{2,1,0:T(8,128)(2,1)} %all-gather.11.cloned.1.call-done, bf16[384,8192]{1,0:T(8,128)(2,1)} %all-gather.7.cloned.1.call-done, f32[8192]{0:T(1024)S(1)} %bitcast.79, f32[384]{0:T(512)S(1)} %add_rsqrt_fusion), kind=kOutput, calls=%fused_computation.32 | convolution fusion | flops 6455427072 | bytes 23889408 | tf_op jit(solution)/shard_map/dot_general | solution.py:56
  363.6 2.8 gather_fusion.4
  366.4 1.3 broadcast_select_fusion
  367.7 0.0 all-to-all-done
  367.7 3.6 all-to-all-start.3
  371.3 0.0 collective-permute-done.1
  371.3 0.0 collective-permute-done.2
  371.4 0.1 collective-permute-start
  371.5 2.6 or_and_fusion
  374.1 0.0 collective-permute-done
  374.1 0.8 fusion.56
  374.9 15.8 %all-to-all-done.3 = bf16[4,192,1024]{2,1,0:T(8,128)(2,1)S(1)} async-done(((bf16[4,192,1024]{2,1,0:T(8,128)(2,1)}), bf16[4,192,1024]{2,1,0:T(8,128)(2,1)S(1)}, u32[]{:S(2)}, u32[]{:S(2)}) %all-to-all-start.3) | async-done | bytes 1572896 | tf_op jit(solution)/shard_map/all_to_all | solution.py:77
  390.7 0.4 copy.25
  391.1 20.6 %fusion.57 = (f32[8,768]{1,0:T(8,128)S(1)}, f32[8,768,1536]{1,2,0:T(8,128)}) fusion(pred[768,1536]{0,1:T(8,128)(4,1)} %or_and_fusion, bf16[768,8,128]{2,1,0:T(8,128)(2,1)S(1)} %bitcast.71, bf16[768,128]{1,0:T(8,128)(2,1)} %get-tuple-element.14, bf16[768,128]{1,0:T(8,128)(2,1)S(1)} %get-tuple-element.12), kind=kOutput, calls=%fused_computation.87 | convolution fusion | flops 2454455808 | bytes 40919040 | tf_op jit(solution)/shard_map/sub | solution.py:102
  411.7 13.2 %fusion.18 = bf16[768,8,128]{0,2,1:T(8,128)(2,1)S(1)} fusion(f32[8,768,1536]{1,2,0:T(8,128)} %get-tuple-element.20, f32[8,768]{1,0:T(8,128)S(1)} %get-tuple-element.19, bf16[768,128]{1,0:T(8,128)(2,1)S(1)} %copy-done.3, bf16[768,128]{1,0:T(8,128)(2,1)S(1)} %get-tuple-element.11), kind=kOutput, calls=%fused_computation.31 | convolution fusion | flops 2436366336 | bytes 39739392 | tf_op jit(solution)/shard_map/hqk,kd->qhd/dot_general | solution.py:104
  424.9 1.2 copy.20
  426.1 2.1 all_to_all.40
  428.1 4.3 all-to-all-start.4
  432.5 18.8 %all-to-all-done.4 = bf16[4,192,1024]{2,1,0:T(8,128)(2,1)} async-done(((bf16[4,192,1024]{2,1,0:T(8,128)(2,1)}), bf16[4,192,1024]{2,1,0:T(8,128)(2,1)}, u32[]{:S(2)}, u32[]{:S(2)}) %all-to-all-start.4) | async-done | bytes 1572896 | tf_op jit(solution)/shard_map/all_to_all | solution.py:106
  451.3 6.3 %gather_fusion.5 = bf16[768,1024]{1,0:T(8,128)(2,1)} fusion(bf16[768,1024]{1,0:T(8,128)(2,1)} %bitcast.14, s32[1024]{0:T(1024)S(1)} %pad_clamp_fusion), kind=kCustom, calls=%fused_computation.5 | custom fusion | bytes 3148800 | tf_op jit(solution)/shard_map/gather | solution.py:108
  457.6 2.7 bitcast_select_fusion.4
  (28 shorter events, 0.2 us)
Async XLA Ops:
  6.5 8.5 %copy-start = (bf16[768,2048]{1,0:T(8,128)(2,1)S(1)}, bf16[768,2048]{1,0:T(8,128)(2,1)}, u32[]{:S(2)}) copy-start(bf16[768,2048]{1,0:T(8,128)(2,1)} %param.7) | copy-start | bytes 9437188
  6.5 129.9 %all-gather.7.cloned.1.call-start = ((), (), s32[]{:S(2)}) async-start(), calls=%async_computation.5 | async-start | bytes 7864320 | tf_op jit(solution)/shard_map/all_gather | solution.py:44
  18.2 170.8 %all-gather.9.cloned.1.call-start = ((), (), s32[]{:S(2)}) async-start(), calls=%async_computation.6 | async-start | bytes 5242880 | tf_op jit(solution)/shard_map/all_gather | solution.py:53
  20.6 9.2 %copy-start.2 = (s32[768]{0:T(1024)S(1)}, s32[768]{0:T(1024)}, u32[]{:S(2)}) copy-start(s32[768]{0:T(1024)} %param.9) | copy-start | bytes 9220
  20.6 330.8 %all-gather.11.cloned.1.call-start = ((), (), s32[]{:S(2)}) async-start(), calls=%async_computation.7 | async-start | bytes 20971520 | tf_op jit(solution)/shard_map/all_gather | solution.py:52
  33.0 156.1 %copy-start.4 = (f32[1,8192]{1,0:T(1,128)S(1)}, f32[1,8192]{1,0:T(1,128)}, u32[]{:S(2)}) copy-start(f32[1,8192]{1,0:T(1,128)} %param.11) | copy-start | bytes 98308
  33.7 9.7 %all-to-all-start.2 = ((s32[4,192,1]{1,2,0:T(1,128)}), s32[4,192,1]{1,2,0:T(1,128)S(1)}, u32[]{:S(2)}, u32[]{:S(2)}) async-start(s32[4,192,1]{1,2,0:T(1,128)} %all_to_all.44), calls=%async_computation.2 | async-start | bytes 8192 | tf_op jit(solution)/shard_map/all_to_all | solution.py:80
  43.4 7.9 %all-to-all-start.1 = ((s32[4,192,1]{1,2,0:T(1,128)}), s32[4,192,1]{1,2,0:T(1,128)S(1)}, u32[]{:S(2)}, u32[]{:S(2)}) async-start(s32[4,192,1]{1,2,0:T(1,128)} %all_to_all.43), calls=%async_computation.1 | async-start | bytes 8192 | tf_op jit(solution)/shard_map/all_to_all | solution.py:79
  51.4 320.0 %collective-permute-start.1 = (s32[768]{0:T(1024)S(1)}, s32[768]{0:T(1024)S(1)}, u32[]{:S(2)}, u32[]{:S(2)}) collective-permute-start(s32[768]{0:T(1024)S(1)} %eq.60), channel_id=1, source_target_pairs={{0,16},{16,0},{1,17},{17,1},{2,18},{18,2},{3,19},{19,3},{4,20},{20... | collective-permute-start | bytes 9224 | tf_op jit(solution)/shard_map/ppermute | solution.py:18
  51.4 320.0 %collective-permute-start.2 = (s32[768]{0:T(1024)S(1)}, s32[768]{0:T(1024)S(1)}, u32[]{:S(2)}, u32[]{:S(2)}) collective-permute-start(s32[768]{0:T(1024)S(1)} %all_to_all.38), channel_id=1, source_target_pairs={{0,16},{16,0},{1,17},{17,1},{2,18},{18,2},{3,19},{19,3},{4,20},{20... | collective-permute-start | bytes 9224 | tf_op jit(solution)/shard_map/ppermute | solution.py:18
  198.5 169.2 %all-to-all-start = ((bf16[4,192,256]{2,1,0:T(8,128)(2,1)}), bf16[4,192,256]{2,1,0:T(8,128)(2,1)S(1)}, u32[]{:S(2)}, u32[]{:S(2)}) async-start(bf16[4,192,256]{2,1,0:T(8,128)(2,1)} %broadcast_select_fusion.1), calls=%async_computation | async-start | bytes 786432 | tf_op jit(solution)/shard_map/all_to_all | solution.py:78
  367.7 22.9 %all-to-all-start.3 = ((bf16[4,192,1024]{2,1,0:T(8,128)(2,1)}), bf16[4,192,1024]{2,1,0:T(8,128)(2,1)S(1)}, u32[]{:S(2)}, u32[]{:S(2)}) async-start(bf16[4,192,1024]{2,1,0:T(8,128)(2,1)} %broadcast_select_fusion), calls=%async_computation.3 | async-start | bytes 3145728 | tf_op jit(solution)/shard_map/all_to_all | solution.py:77
  371.4 2.7 collective-permute-start
  391.1 20.6 %copy-start.3 = (bf16[768,128]{1,0:T(8,128)(2,1)S(1)}, bf16[768,128]{1,0:T(8,128)(2,1)}, u32[]{:S(2)}) copy-start(bf16[768,128]{1,0:T(8,128)(2,1)} %get-tuple-element.13) | copy-start | bytes 589828
  428.1 23.2 %all-to-all-start.4 = ((bf16[4,192,1024]{2,1,0:T(8,128)(2,1)}), bf16[4,192,1024]{2,1,0:T(8,128)(2,1)}, u32[]{:S(2)}, u32[]{:S(2)}) async-start(bf16[4,192,1024]{2,1,0:T(8,128)(2,1)} %all_to_all.40), calls=%async_computation.4 | async-start | bytes 3145728 | tf_op jit(solution)/shard_map/all_to_all | solution.py:106
  451.3 9.0 %copy-start.1 = (bf16[768,2048]{1,0:T(8,128)(2,1)S(1)}, bf16[768,2048]{1,0:T(8,128)(2,1)}, u32[]{:S(2)}) copy-start(bf16[768,2048]{1,0:T(8,128)(2,1)} %param.7) | copy-start | bytes 9437188
Sparse Core Ops, SparseCore 0:
  18.3 118.0 all-gather.6
  138.2 50.7 all-gather.8
  190.9 160.4 all-gather.10
where the time goes:
time: 467 us
  waiting for transfers between devices  326 us (70%)
  matrix products  51.8 us (11%)
  local copies, waits for them, and re-layouts  38.6 us (8%)
  starting transfers between devices  20.6 us (4%)
  other arithmetic  16.6 us (4%)
  between operations  13.4 us (3%)
    all_gather x1, waiting for transfers between devices, local(): lax.all_gather(query_local, 'grp', axis=0, tiled=True)  149 us
    all_gather x1, waiting for transfers between devices, local(): features = lax.all_gather(chosen, 'tp', axis=1, tiled=True)  84.5 us
    all_gather x1, waiting for transfers between devices, local(): lax.all_gather(pair_part, 'grp', axis=0, tiled=True)  48.5 us
    sub x1, matrix products, local(): powered = jnp.exp(scores - row_max)  20.6 us
    all_to_all x1, waiting for transfers between devices, local(): lax.all_to_all(mixed_rows, 'grp', split_axis=0, concat_axis=0, tiled=True)  18.8 us
    dot_general x2, matrix products, local(): jnp.dot(normed, weight_rows, preferred_element_type=jnp.float32)  18 us
    all_to_all x1, waiting for transfers between devices, local(): lax.all_to_all(query_send, 'grp', split_axis=0, concat_axis=0, tiled=True)  15.8 us
    dot_general x1, matrix products, local(): jnp.einsum('hqk,kd->qhd', weights, value_rows, preferred_element_type=jnp...  13.2 us
  transfers between devices with their start and end apart: 11, of which 7 were waited for; matrix products, arithmetic and copies ran while one was open for 10% of the time, Pallas kernels for 0%

commit v1 on v0

v1 whole, which is shorter than its diff:
```python
import math

import jax
import jax.numpy as jnp
from jax import lax
from jax.sharding import PartitionSpec as P

HD = 128
EPS = 1e-05
MASKED = -1e30


def swap_tower(value):
    return lax.ppermute(value, "tower", [(0, 1), (1, 0)])


def pick(onehot, rows):
    return jnp.dot(onehot.astype(jnp.bfloat16), rows, preferred_element_type=jnp.float32).astype(
        jnp.bfloat16
    )


def move_tokens(chosen):
    gathered = lax.all_gather(chosen, "tp", axis=0, tiled=False)
    return lax.all_to_all(gathered, "grp", split_axis=0, concat_axis=0, tiled=True)


def to_owner(partial):
    return lax.all_to_all(partial, "grp", split_axis=0, concat_axis=0, tiled=True)


def local(tokens, modality, doc_ids, owner_ids, norm_gain, query_weight, pair_weight):
    groups = lax.axis_size("grp")
    tp_count = lax.axis_size("tp")
    tower = lax.axis_index("tower")
    group = lax.axis_index("grp")
    tp_rank = lax.axis_index("tp")
    tok, width = tokens.shape
    half = tok // 2
    slot_count = tok // groups
    head_cols = query_weight.shape[2]
    pair_heads = pair_weight.shape[2] // (2 * HD)
    own_head = tp_rank // (tp_count // pair_heads)
    features = width * tp_count
    bf16, f32, i32 = jnp.bfloat16, jnp.float32, jnp.int32

    values = tokens.astype(f32)
    code = (doc_ids * groups + owner_ids) * 2 + modality
    facts = jnp.stack([code.astype(f32), jnp.sum(values * values, axis=1)])
    facts = lax.all_gather(facts, ("grp", "tp"), axis=0, tiled=False)
    facts = facts.reshape(groups, tp_count, 2, tok)
    codes = facts[:, 0, 0, :].astype(i32)
    mods = codes % 2
    owners = (codes // 2) % groups
    squares = jnp.sum(lax.dynamic_index_in_dim(facts, group, 0, False)[:, 1, :], axis=0)
    inverse_rms = lax.rsqrt(squares / features + EPS)

    where_i = jnp.arange(tok, dtype=i32)
    before = (where_i[None, :] < where_i[:, None])[None]
    owner_rank = jnp.sum(((owners[:, None, :] == owners[:, :, None]) & before).astype(i32), axis=2)
    mod_rank = jnp.sum(((mods[:, None, :] == mods[:, :, None]) & before).astype(i32), axis=2)
    slots = owners * slot_count + owner_rank
    packed = mods * half + mod_rank
    at_slot = slots[:, None, :] == where_i[None, :, None]
    packed_of_slot = jnp.sum(jnp.where(at_slot, packed[:, None, :], 0), axis=2)

    slots_here = lax.dynamic_index_in_dim(slots, group, 0, False)
    packed_here = lax.dynamic_index_in_dim(packed, group, 0, False)

    gain = lax.dynamic_slice_in_dim(norm_gain[0], tp_rank * width, width, 0)
    normed = (values * inverse_rms[:, None] * gain[None, :]).astype(bf16)
    choose = packed_here[None, :] == (tower * half + jnp.arange(half, dtype=i32))[:, None]
    chosen = pick(choose, normed)
    arrived = move_tokens(chosen).reshape(groups * half, width)

    pair_part = lax.dynamic_slice_in_dim(pair_weight[0], own_head * 2 * HD, 2 * HD, 1)
    half_cols = head_cols // 2
    query_part = jnp.dot(arrived, query_weight[0], preferred_element_type=f32).astype(bf16)
    pair_part = jnp.dot(arrived, pair_part, preferred_element_type=f32).astype(bf16)
    query_keep = lax.dynamic_slice_in_dim(query_part, tower * half_cols, half_cols, 1)
    query_give = lax.dynamic_slice_in_dim(query_part, (1 - tower) * half_cols, half_cols, 1)
    keep = jnp.concatenate([query_keep, pair_part], axis=1)
    got = swap_tower(jnp.concatenate([query_give, pair_part], axis=1))
    cols = half_cols + 2 * HD
    keep = keep.reshape(groups, half, cols)
    got = got.reshape(groups, half, cols)
    own_first = jnp.concatenate([keep, got], axis=1)
    position = packed_of_slot - tower * half
    position = jnp.where(position < 0, position + tok, position)
    expand = (position[:, :, None] == where_i[None, None, :]).astype(bf16)
    slotted = jnp.einsum("gsp,gpc->gsc", expand, own_first, preferred_element_type=f32).astype(bf16)
    by_owner = slotted.reshape(groups, groups, slot_count, cols).transpose(1, 0, 2, 3)
    parts = to_owner(by_owner.reshape(groups, tok, cols))
    rows = jnp.sum(parts.astype(f32), axis=0).astype(bf16)

    mine = group * slot_count + jnp.arange(slot_count, dtype=i32)
    at_mine = slots[:, None, :] == mine[None, :, None]
    code_mine = jnp.sum(jnp.where(at_mine, codes[:, None, :], 0), axis=2).reshape(tok)
    place_mine = jnp.sum(jnp.where(at_mine, where_i[None, None, :], 0), axis=2)
    place_mine = (place_mine + tok * jnp.arange(groups, dtype=i32)[:, None]).reshape(tok)
    image = code_mine % 2 == 1
    doc = code_mine // (2 * groups)
    allowed = (doc[:, None] == doc[None, :]) & (
        (place_mine[None, :] <= place_mine[:, None]) | (image[:, None] & image[None, :])
    )
    heads = half_cols // HD
    queries = rows[:, :half_cols].reshape(tok, heads, HD)
    keys = rows[:, half_cols : half_cols + HD]
    vals = rows[:, half_cols + HD :]
    scores = jnp.einsum("qhd,kd->hqk", queries, keys, preferred_element_type=f32) * (
        1.0 / math.sqrt(HD)
    )
    scores = jnp.where(allowed[None], scores, MASKED)
    powered = jnp.exp(scores - jnp.max(scores, axis=2, keepdims=True))
    weights = (powered / jnp.sum(powered, axis=2, keepdims=True)).astype(bf16)
    mixed = jnp.einsum("hqk,kd->qhd", weights, vals, preferred_element_type=f32)
    mixed = mixed.astype(bf16).reshape(tok, half_cols)

    returned = lax.all_to_all(mixed, "grp", split_axis=0, concat_axis=0, tiled=True)
    other = swap_tower(returned)
    left = jnp.where(tower == 0, returned, other)
    right = jnp.where(tower == 0, other, returned)
    in_tower = modality == tower
    place = (slots_here[:, None] == where_i[None, :]) & in_tower[:, None]
    result = pick(place, jnp.concatenate([left, right], axis=1))
    return result[None]


def solution(mesh):
    in_specs = (
        P("grp", "tp"),
        P("grp"),
        P("grp"),
        P("grp"),
        P("tower", None),
        P("tower", "grp", "tp"),
        P("tower", "grp", None),
    )
    out_specs = P("tower", "grp", "tp")
    return jax.shard_map(local, mesh=mesh, in_specs=in_specs, out_specs=out_specs, check_vma=False)
```

time: 467 us -> 383 us (0.82)
  waiting for transfers between devices: 326 us -> 237 us
  blocking collectives: 0 us -> 56.8 us
  local copies, waits for them, and re-layouts: 38.6 us -> 11 us
  matrix products: 51.8 us -> 36 us
  starting transfers between devices: 20.6 us -> 10.6 us
    all_gather x3 -> x1, waiting for transfers between devices: 282 us -> 112 us  [move_tokens(): gathered = lax.all_gather(chosen, 'tp', axis=0, tiled=False)]
    all_to_all x5 -> x2, waiting for transfers between devices: 42.9 us -> 122 us  [the longest x1 70.1 us: move_tokens(): lax.all_to_all(gathered, 'grp', split_axis=0, concat_axis=0, tiled=True)]
    all_gather x0 -> x1, blocking collectives: none -> 43.3 us  [local(): facts = lax.all_gather(facts, ('grp', 'tp'), axis=0, tiled=False)]
    gather x6 -> x0, local copies, waits for them, and re-layouts: 23.1 us -> none  [the longest x1 6.3 us: local(): result = jnp.where(in_tower[:, None], returned[safe_dest], zero_value)]
    sub x1, matrix products: 20.6 us -> 5.69 us  [local(): powered = jnp.exp(scores - jnp.max(scores, axis=2, keepdims=True))]
    all_to_all x0 -> x1, blocking collectives: none -> 13.5 us  [local(): lax.all_to_all(mixed, 'grp', split_axis=0, concat_axis=0, tiled=True)]
    reshape x0 -> x4, local copies, waits for them, and re-layouts: none -> 9.39 us  [the longest x1 4.28 us: local(): got = got.reshape(groups, half, cols)]
    all_to_all x5 -> x2, starting transfers between devices: 20 us -> 10.6 us  [the longest x1 5.42 us: move_tokens(): lax.all_to_all(gathered, 'grp', split_axis=0, concat_axis=0, tiled=True)]
  transfers between devices with their start and end apart: 11 -> 5, of which waited for: 7 -> 5; matrix products, arithmetic and copies ran while one was open for 10% -> 1% of each run, Pallas kernels for 0% -> 0%
where the time goes in v1:
time: 383 us
  waiting for transfers between devices  237 us (62%)
  blocking collectives  56.8 us (15%)
  matrix products  36 us (9%)
  other arithmetic  17.8 us (5%)
  between operations  13.7 us (4%)
  local copies, waits for them, and re-layouts  11 us (3%)
  starting transfers between devices  10.6 us (3%)
    all_gather x1, waiting for transfers between devices, move_tokens(): gathered = lax.all_gather(chosen, 'tp', axis=0, tiled=False)  112 us
    all_to_all x1, waiting for transfers between devices, move_tokens(): lax.all_to_all(gathered, 'grp', split_axis=0, concat_axis=0, tiled=True)  70.1 us
    all_to_all x1, waiting for transfers between devices, to_owner(): lax.all_to_all(partial, 'grp', split_axis=0, concat_axis=0, tiled=True)  51.4 us
    all_gather x1, blocking collectives, local(): facts = lax.all_gather(facts, ('grp', 'tp'), axis=0, tiled=False)  43.3 us
    all_to_all x1, blocking collectives, local(): lax.all_to_all(mixed, 'grp', split_axis=0, concat_axis=0, tiled=True)  13.5 us
    dot_general x1, matrix products, local(): jnp.dot(arrived, query_weight[0], preferred_element_type=f32).astype(bf16)  10.2 us
  transfers between devices with their start and end apart: 5, of which 5 were waited for; matrix products, arithmetic and copies ran while one was open for 1% of the time, Pallas kernels for 0%

profile of v1, /device:TPU:0, one launch (start us, length us, event | category | flops | bytes accessed | tf_op | source)
XLA Modules:
  0.0 382.5 jit_solution(9220705877030252928)
XLA Ops:
  6.5 0.0 copy-start
  6.5 0.0 copy-start.2
  6.5 0.0 copy-start.5
  6.5 0.0 copy-start.4
  6.5 0.0 copy-start.6
  6.5 0.0 all-gather.5.cloned.1.call-start
  6.6 1.0 iota_compare_fusion.6
  7.6 2.7 fusion.3
  10.3 0.0 copy-done.5
  10.3 0.0 copy-done.4
  10.4 0.0 copy-done.6
  10.4 43.3 %all-gather.2 = f32[16,2,768]{2,1,0:T(2,128)S(1)} all-gather(f32[1,2,768]{2,1,0:T(2,128)S(1)} %maximum_bitcast_fusion), channel_id=2, replica_groups=mesh['tower'=2,'tp'=4,'grp'=4] {'grp','tp'}, dimensions={0}, use_global_device_ids=true | all-gather | bytes 104448 | tf_op jit(solution)/shard_map/all_gather | solution.py:50
  53.8 5.2 %convert_reduce_fusion = (s32[4,768]{1,0:T(4,128)S(1)}, s32[4,768]{1,0:T(4,128)S(1)}) fusion(s32[4,768]{1,0:T(4,128)S(1)} %get-tuple-element.16, pred[768,768]{1,0:T(8,128)(4,1)} %iota_compare_fusion.6, s32[4,768]{1,0:T(4,128)S(1)} %get-tuple-element.15), kind=kLoop, calls=%fused_computation.6 | loop fusion | flops 18868224 | bytes 638976 | tf_op jit(solution)/shard_map/reduce_sum | solution.py:61
  59.2 0.0 copy-done
  59.2 0.0 copy-done.2
  59.2 2.8 fusion.28
  62.0 0.0 all-gather.5.cloned.1.call-update
  62.0 111.6 %all-gather.5.cloned.1.call-done = bf16[1536,2048]{1,0:T(8,128)(2,1)} async-done(((bf16[384,2048]{1,0:T(8,128)(2,1)}), bf16[1536,2048]{1,0:T(8,128)(2,1)}) %all-gather.5.cloned.1.call-update) | async-done | bytes 6291472 | tf_op jit(solution)/shard_map/all_gather | solution.py:24
  173.6 5.4 %all-to-all-start = ((bf16[4,384,2048]{2,1,0:T(8,128)(2,1)}), bf16[4,384,2048]{2,1,0:T(8,128)(2,1)}, u32[]{:S(2)}, u32[]{:S(2)}) async-start(bf16[4,384,2048]{2,1,0:T(8,128)(2,1)} %bitcast.69), calls=%async_computation | async-start | bytes 12582912 | tf_op jit(solution)/shard_map/all_to_all | solution.py:25
  179.1 70.1 %all-to-all-done = bf16[4,384,2048]{2,1,0:T(8,128)(2,1)} async-done(((bf16[4,384,2048]{2,1,0:T(8,128)(2,1)}), bf16[4,384,2048]{2,1,0:T(8,128)(2,1)}, u32[]{:S(2)}, u32[]{:S(2)}) %all-to-all-start) | async-done | bytes 6291488 | tf_op jit(solution)/shard_map/all_to_all | solution.py:25
  249.2 10.2 %fusion.16 = bf16[1536,1024]{0,1:T(8,128)(2,1)S(1)} fusion(bf16[1536,2048]{1,0:T(8,128)(2,1)} %bitcast.6, bf16[1,2048,1024]{2,1,0:T(8,128)(2,1)} %param.12), kind=kOutput, calls=%fused_computation.26 | convolution fusion | flops 6444023808 | bytes 13631488 | tf_op jit(solution)/shard_map/dot_general | solution.py:78
  259.4 4.9 %convolution_convert_fusion = bf16[1536,256]{0,1:T(8,128)(2,1)S(1)} fusion(bf16[1536,2048]{1,0:T(8,128)(2,1)} %bitcast.6, bf16[1,2048,1024]{2,1,0:T(8,128)(2,1)} %param.13, s32[]{:T(128)S(6)} %select_n.141), kind=kOutput, calls=%fused_computation.37 | convolution fusion | flops 1611005952 | bytes 8126468 | tf_op jit(solution)/shard_map/dot_general | solution.py:79
  264.3 0.2 constant_dynamic-slice_fusion.1
  264.5 1.8 pad_maximum_fusion.1
  266.2 0.0 collective-permute-start
  266.2 1.2 select_reduce_fusion
  267.5 2.5 copy.40
  269.9 0.0 copy-start.3
  269.9 1.2 collective-permute-done
  271.1 4.3 %copy.41 = bf16[1536,768]{1,0:T(8,128)(2,1)} copy(bf16[1536,768]{0,1:T(8,128)(2,1)} %collective-permute-done) | data formatting | bytes 4718592 | tf_op jit(solution)/shard_map/reshape | solution.py:86
  275.4 0.0 copy-done.3
  275.4 5.4 %fusion.25 = bf16[4,768,768]{2,1,0:T(8,128)(2,1)S(1)} fusion(bf16[4,384,768]{2,1,0:T(8,128)(2,1)} %bitcast.73, bf16[4,384,768]{2,1,0:T(8,128)(2,1)S(1)} %bitcast.72, s32[4,768]{1,0:T(4,128)S(1)} %compare_select_fusion.2), kind=kOutput, calls=%fused_computation.33 | convolution fusion | flops 3638034432 | bytes 9449472 | tf_op jit(solution)/shard_map/gsp,gpc->gsc/dot_general | solution.py:91
  280.8 2.6 copy.31
  283.4 5.2 %all-to-all-start.1 = ((bf16[4,768,768]{2,1,0:T(8,128)(2,1)}), bf16[4,768,768]{2,1,0:T(8,128)(2,1)}, u32[]{:S(2)}, u32[]{:S(2)}) async-start(bf16[4,768,768]{2,1,0:T(8,128)(2,1)} %bitcast.68), calls=%async_computation.1 | async-start | bytes 9437184 | tf_op jit(solution)/shard_map/all_to_all | solution.py:29
  288.6 0.7 fusion.31
  289.2 0.1 reshape.392
  289.3 0.1 broadcast_add_fusion
  289.4 0.1 add.187
  289.5 1.0 or_and_fusion
  290.5 51.4 %all-to-all-done.1 = bf16[4,768,768]{2,1,0:T(8,128)(2,1)} async-done(((bf16[4,768,768]{2,1,0:T(8,128)(2,1)}), bf16[4,768,768]{2,1,0:T(8,128)(2,1)}, u32[]{:S(2)}, u32[]{:S(2)}) %all-to-all-start.1) | async-done | bytes 4718624 | tf_op jit(solution)/shard_map/all_to_all | solution.py:29
  341.9 3.8 reduce_sum.89
  345.7 0.1 slice.24
  345.7 0.3 copy.32
  346.0 5.7 %fusion.68 = (f32[4,768]{1,0:T(4,128)S(1)}, f32[4,768,768]{1,2,0:T(8,128)}) fusion(pred[768,768]{0,1:T(8,128)(4,1)S(1)} %or_and_fusion, bf16[768,4,128]{0,2,1:T(8,128)(2,1)S(1)} %bitcast.74, bf16[768,768]{1,0:T(8,128)(2,1)S(1)} %reduce_sum.89), kind=kOutput, calls=%fused_computation.111 | convolution fusion | flops 613417728 | bytes 11022336 | tf_op jit(solution)/shard_map/sub | solution.py:114
  351.7 4.5 %fusion.48 = bf16[768,4,128]{0,2,1:T(8,128)(2,1)S(1)} fusion(f32[4,768,768]{1,2,0:T(8,128)} %get-tuple-element.18, f32[4,768]{1,0:T(4,128)S(1)} %get-tuple-element.17, bf16[768,768]{1,0:T(8,128)(2,1)S(1)} %reduce_sum.89), kind=kOutput, calls=%fused_computation.51 | convolution fusion | flops 609091584 | bytes 10432512 | tf_op jit(solution)/shard_map/hqk,kd->qhd/dot_general | solution.py:116
  356.2 0.6 copy.36
  356.8 0.3 all_to_all.16
  357.1 13.5 %all_to_all.22 = bf16[4,192,512]{2,1,0:T(8,128)(2,1)S(1)} all-to-all(bf16[4,192,512]{2,1,0:T(8,128)(2,1)S(1)} %all_to_all.16), channel_id=1, replica_groups=mesh['tower'=2,'tp'=4,'grp'=4] {'grp'}, dimensions={0} | all-to-all | bytes 1572864 | tf_op jit(solution)/shard_map/all_to_all | solution.py:119
  370.6 0.0 collective-permute-start.1
  370.7 2.2 collective-permute-done.1
  372.9 0.2 broadcast_select_fusion.1
  373.1 0.0 copy-start.1
  373.1 2.6 fusion.42
  375.7 0.0 copy-done.1
  (21 shorter events, 0.2 us)
Async XLA Ops:
  6.5 52.6 %copy-start = (f32[1,8192]{1,0:T(1,128)S(1)}, f32[1,8192]{1,0:T(1,128)}, u32[]{:S(2)}) copy-start(f32[1,8192]{1,0:T(1,128)} %param.11) | copy-start | bytes 98308
  6.5 52.7 %copy-start.2 = (bf16[768,2048]{1,0:T(8,128)(2,1)S(1)}, bf16[768,2048]{1,0:T(8,128)(2,1)}, u32[]{:S(2)}) copy-start(bf16[768,2048]{1,0:T(8,128)(2,1)} %param.7) | copy-start | bytes 9437188
  6.5 3.8 copy-start.5
  6.5 3.8 copy-start.4
  6.5 3.8 copy-start.6
  6.5 167.1 %all-gather.5.cloned.1.call-start = ((), (), s32[]{:S(2)}) async-start(), calls=%async_computation.3 | async-start | bytes 7864320 | tf_op jit(solution)/shard_map/all_gather | solution.py:24
  173.6 75.6 %all-to-all-start = ((bf16[4,384,2048]{2,1,0:T(8,128)(2,1)}), bf16[4,384,2048]{2,1,0:T(8,128)(2,1)}, u32[]{:S(2)}, u32[]{:S(2)}) async-start(bf16[4,384,2048]{2,1,0:T(8,128)(2,1)} %bitcast.69), calls=%async_computation | async-start | bytes 12582912 | tf_op jit(solution)/shard_map/all_to_all | solution.py:25
  266.2 4.9 %collective-permute-start = (bf16[1536,768]{0,1:T(8,128)(2,1)}, bf16[1536,768]{0,1:T(8,128)(2,1)}, u32[]{:S(2)}, u32[]{:S(2)}) collective-permute-start(bf16[1536,768]{0,1:T(8,128)(2,1)} %get-tuple-element.14), channel_id=1, source_target_pairs={{0,16},{16,0},{1,17},{17,1},{2,18},{18,2},{3,19},{19,3},{4,20},{20... | collective-permute-start | bytes 7077896 | tf_op jit(solution)/shard_map/ppermute | solution.py:14
  269.9 5.5 %copy-start.3 = (bf16[1536,768]{1,0:T(8,128)(2,1)S(1)}, bf16[1536,768]{1,0:T(8,128)(2,1)}, u32[]{:S(2)}) copy-start(bf16[1536,768]{1,0:T(8,128)(2,1)} %copy.40) | copy-start | bytes 7077892
  283.4 58.5 %all-to-all-start.1 = ((bf16[4,768,768]{2,1,0:T(8,128)(2,1)}), bf16[4,768,768]{2,1,0:T(8,128)(2,1)}, u32[]{:S(2)}, u32[]{:S(2)}) async-start(bf16[4,768,768]{2,1,0:T(8,128)(2,1)} %bitcast.68), calls=%async_computation.1 | async-start | bytes 9437184 | tf_op jit(solution)/shard_map/all_to_all | solution.py:29
  370.6 2.3 collective-permute-start.1
  373.1 2.6 copy-start.1
Sparse Core Ops, SparseCore 0:
  62.1 111.4 all-gather.4

commit v2 on v1

--- a/solution.py
+++ b/solution.py
@@ -1,8 +1,11 @@
+import functools
 import math
 
 import jax
 import jax.numpy as jnp
 from jax import lax
+from jax.experimental import pallas as pl
+from jax.experimental.pallas import tpu as pltpu
 from jax.sharding import PartitionSpec as P
 
 HD = 128
@@ -20,9 +23,219 @@
     )
 
 
-def move_tokens(chosen):
-    gathered = lax.all_gather(chosen, "tp", axis=0, tiled=False)
-    return lax.all_to_all(gathered, "grp", split_axis=0, concat_axis=0, tiled=True)
+MESH = pl.DeviceIdType.MESH
+
+
+def greet(devices):
+    barrier = pltpu.get_barrier_semaphore()
+    for present, device in devices:
+
+        @pl.when(present)
+        def _(device=device):
+            pl.semaphore_signal(barrier, inc=1, device_id=device, device_id_type=MESH)
+
+    pl.semaphore_wait(barrier, sum(jnp.asarray(present, jnp.int32) for present, _ in devices))
+
+
+def others(axis, count):
+    me = lax.axis_index(axis)
+    return [(True, {axis: lax.rem(me + k, count)}) for k in range(1, count)]
+
+
+def facts_kernel(groups, tp_count, facts, by_group, by_block, send_sem, group_sem, block_sem):
+    group, block = lax.axis_index("grp"), lax.axis_index("tp")
+    greet(others("grp", groups) + others("tp", tp_count))
+    sent = []
+    for k in range(1, groups):
+        sent.append(
+            pltpu.make_async_remote_copy(
+                src_ref=facts,
+                dst_ref=by_group.at[group],
+                send_sem=send_sem.at[k - 1],
+                recv_sem=group_sem.at[group],
+                device_id={"grp": lax.rem(group + k, groups)},
+                device_id_type=MESH,
+            )
+        )
+    for k in range(1, tp_count):
+        sent.append(
+            pltpu.make_async_remote_copy(
+                src_ref=facts,
+                dst_ref=by_block.at[block],
+                send_sem=send_sem.at[groups + k - 2],
+                recv_sem=block_sem.at[block],
+                device_id={"tp": lax.rem(block + k, tp_count)},
+                device_id_type=MESH,
+            )
+        )
+    for copy in sent:
+        copy.start()
+    by_group[group] = facts[...]
+    by_block[block] = facts[...]
+    for k in range(1, groups):
+        source = lax.rem(group + k, groups)
+        pltpu.make_async_copy(facts, by_group.at[source], group_sem.at[source]).wait()
+    for k in range(1, tp_count):
+        source = lax.rem(block + k, tp_count)
+        pltpu.make_async_copy(facts, by_block.at[source], block_sem.at[source]).wait()
+    for copy in sent:
+        copy.wait_send()
+
+
+def share_facts(facts, groups, tp_count):
+    vmem = pl.BlockSpec(memory_space=pltpu.VMEM)
+    return pl.pallas_call(
+        functools.partial(facts_kernel, groups, tp_count),
+        out_shape=[
+            jax.ShapeDtypeStruct((groups,) + facts.shape, facts.dtype),
+            jax.ShapeDtypeStruct((tp_count,) + facts.shape, facts.dtype),
+        ],
+        in_specs=[vmem],
+        out_specs=[vmem, vmem],
+        scratch_shapes=[
+            pltpu.SemaphoreType.DMA((groups + tp_count - 2,)),
+            pltpu.SemaphoreType.DMA((groups,)),
+            pltpu.SemaphoreType.DMA((tp_count,)),
+        ],
+        compiler_params=pltpu.CompilerParams(collective_id=1, has_side_effects=True),
+        name="share_facts",
+    )(facts)
+
+
+def tokens_kernel(
+    groups, count, chunks, chosen, out, held, own_sem, line_send, line_recv, cross_send, cross_recv
+):
+    group, me = lax.axis_index("grp"), lax.axis_index("tp")
+    rows = chosen.shape[0] // chunks
+    has_left, has_right = me > 0, me < count - 1
+    left, right = jnp.maximum(me - 1, 0), jnp.minimum(me + 1, count - 1)
+    greet([(has_left, {"tp": left}), (has_right, {"tp": right})] + others("grp", groups))
+
+    def part(chunk):
+        return pl.ds(pl.multiple_of(chunk * rows, rows), rows)
+
+    def hop(source, chunk, way, own):
+        src = chosen if own else held.at[source]
+        return pltpu.make_async_remote_copy(
+            src_ref=src.at[part(chunk)],
+            dst_ref=held.at[source, part(chunk)],
+            send_sem=line_send.at[way, source, chunk],
+            recv_sem=line_recv.at[source, chunk],
+            device_id={"tp": left if way == 0 else right},
+            device_id_type=MESH,
+        )
+
+    def cross(source, chunk, own):
+        src = chosen if own else held.at[source]
+        return pltpu.make_async_remote_copy(
+            src_ref=src.at[part(chunk)],
+            dst_ref=out.at[group, part(chunk)],
+            send_sem=cross_send.at[source, chunk],
+            recv_sem=cross_recv.at[group, chunk],
+            device_id={"grp": source},
+            device_id_type=MESH,
+        )
+
+    def keep(source, chunk, own):
+        src = chosen if own else held.at[source]
+        return pltpu.make_async_copy(
+            src.at[part(chunk)], out.at[group, part(chunk)], own_sem.at[chunk]
+        )
+
+    def pass_on(source, chunk, own):
+        @pl.when(source == group)
+        def _():
+            keep(source, chunk, own).start()
+
+        @pl.when(source != group)
+        def _():
+            cross(source, chunk, own).start()
+
+    def start_own(chunk):
+        @pl.when(has_left)
+        def _():
+            hop(me, chunk, 0, True).start()
+
+        @pl.when(has_right)
+        def _():
+            hop(me, chunk, 1, True).start()
+
+        pass_on(me, chunk, True)
+
+    def arrive(source, chunk, way, more):
+        hop(source, chunk, way, False).wait_recv()
+
+        @pl.when(more)
+        def _():
+            hop(source, chunk, way, False).start()
+
+        pass_on(source, chunk, False)
+
+    start_own(0)
+
+    @pl.loop(0, chunks)
+    def _(chunk):
+        @pl.when(chunk + 1 < chunks)
+        def _():
+            start_own(chunk + 1)
+
+        for k in range(1, count):
+
+            @pl.when(me + k < count)
+            def _():
+                arrive(me + k, chunk, 0, has_left)
+
+            @pl.when(me - k >= 0)
+            def _():
+                arrive(me - k, chunk, 1, has_right)
+
+    @pl.loop(0, chunks)
+    def _(chunk):
+        for k in range(1, groups):
+            source = lax.rem(group + k, groups)
+            pltpu.make_async_copy(
+                chosen.at[part(chunk)], out.at[source, part(chunk)], cross_recv.at[source, chunk]
+            ).wait()
+        keep(group, chunk, False).wait()
+        for source in range(count):
+
+            @pl.when(source != group)
+            def _():
+                cross(source, chunk, False).wait_send()
+
+            @pl.when((source >= me) & has_left)
+            def _():
+                hop(source, chunk, 0, False).wait_send()
+
+            @pl.when((source <= me) & has_right)
+            def _():
+                hop(source, chunk, 1, False).wait_send()
+
+
+def move_tokens(chosen, groups, tp_count):
+    half, width = chosen.shape
+    chunks = max(1, 24 // tp_count)
+    while half % chunks or (half // chunks) % 16:
+        chunks -= 1
+    vmem = pl.BlockSpec(memory_space=pltpu.VMEM)
+    return pl.pallas_call(
+        functools.partial(tokens_kernel, groups, tp_count, chunks),
+        out_shape=jax.ShapeDtypeStruct((groups, half, width), chosen.dtype),
+        in_specs=[vmem],
+        out_specs=vmem,
+        scratch_shapes=[
+            pltpu.VMEM((tp_count, half, width), chosen.dtype),
+            pltpu.SemaphoreType.DMA((chunks,)),
+            pltpu.SemaphoreType.DMA((2, tp_count, chunks)),
+            pltpu.SemaphoreType.DMA((tp_count, chunks)),
+            pltpu.SemaphoreType.DMA((tp_count, chunks)),
+            pltpu.SemaphoreType.DMA((groups, chunks)),
+        ],
+        compiler_params=pltpu.CompilerParams(
+            collective_id=2, has_side_effects=True, vmem_limit_bytes=40 * 2**20
+        ),
+        name="move_tokens",
+    )(chosen)
 
 
 def to_owner(partial):
@@ -46,13 +259,14 @@
 
     values = tokens.astype(f32)
     code = (doc_ids * groups + owner_ids) * 2 + modality
-    facts = jnp.stack([code.astype(f32), jnp.sum(values * values, axis=1)])
-    facts = lax.all_gather(facts, ("grp", "tp"), axis=0, tiled=False)
-    facts = facts.reshape(groups, tp_count, 2, tok)
-    codes = facts[:, 0, 0, :].astype(i32)
+    squares = jnp.sum(values * values, axis=1)
+    row = jnp.arange(8, dtype=i32)[:, None]
+    facts = jnp.where(row == 0, code.astype(f32)[None, :], jnp.where(row == 1, squares[None, :], 0.0))
+    by_group, by_block = share_facts(facts, groups, tp_count)
+    codes = by_group[:, 0, :].astype(i32)
     mods = codes % 2
     owners = (codes // 2) % groups
-    squares = jnp.sum(lax.dynamic_index_in_dim(facts, group, 0, False)[:, 1, :], axis=0)
+    squares = jnp.sum(by_block[:, 1, :], axis=0)
     inverse_rms = lax.rsqrt(squares / features + EPS)
 
     where_i = jnp.arange(tok, dtype=i32)
@@ -71,7 +285,7 @@
     normed = (values * inverse_rms[:, None] * gain[None, :]).astype(bf16)
     choose = packed_here[None, :] == (tower * half + jnp.arange(half, dtype=i32))[:, None]
     chosen = pick(choose, normed)
-    arrived = move_tokens(chosen).reshape(groups * half, width)
+    arrived = move_tokens(chosen, groups, tp_count).reshape(groups * half, width)
 
     pair_part = lax.dynamic_slice_in_dim(pair_weight[0], own_head * 2 * HD, 2 * HD, 1)
     half_cols = head_cols // 2

time: 383 us -> 268 us (0.70)
  waiting for transfers between devices: 237 us -> 55.3 us
  Pallas kernels: 0 us -> 120 us
  blocking collectives: 56.8 us -> 14.6 us
  between operations: 13.7 us -> 0.34 us
    pallas_call x0 -> x2, Pallas kernels: none -> 120 us  [the longest x1 109 us: move_tokens(): pl.pallas_call(functools.partial(tokens_kernel, groups, tp_count, chunks)...]
    all_gather x1 -> x0, waiting for transfers between devices: 112 us -> none  [move_tokens(): gathered = lax.all_gather(chosen, 'tp', axis=0, tiled=False)]
    all_to_all x1 -> x0, waiting for transfers between devices: 70.1 us -> none  [move_tokens(): lax.all_to_all(gathered, 'grp', split_axis=0, concat_axis=0, tiled=True)]
    all_gather x1 -> x0, blocking collectives: 43.3 us -> none  [local(): facts = lax.all_gather(facts, ('grp', 'tp'), axis=0, tiled=False)]
    all_to_all x1 -> x0, starting transfers between devices: 5.42 us -> none  [move_tokens(): lax.all_to_all(gathered, 'grp', split_axis=0, concat_axis=0, tiled=True)]
    all_to_all x1, starting transfers between devices: 5.15 us -> 9.18 us  [to_owner(): lax.all_to_all(partial, 'grp', split_axis=0, concat_axis=0, tiled=True)]
  transfers between devices with their start and end apart: 5 -> 3, of which waited for: 5 -> 3; matrix products, arithmetic and copies ran while one was open for 1% -> 2% of each run, Pallas kernels for 0% -> 0%
where the time goes in v2:
time: 268 us; the launch traced here: 267 us
  Pallas kernels  120 us (45%)
  waiting for transfers between devices  55.3 us (21%)
  matrix products  33.1 us (12%)
  other arithmetic  21.3 us (8%)
  blocking collectives  14.6 us (5%)
  local copies, waits for them, and re-layouts  13.6 us (5%)
  starting transfers between devices  9.18 us (3%)
    pallas_call x1, Pallas kernels, move_tokens(): pl.pallas_call(functools.partial(tokens_kernel, groups, tp_count, chunks)...  109 us
    all_to_all x1, waiting for transfers between devices, to_owner(): lax.all_to_all(partial, 'grp', split_axis=0, concat_axis=0, tiled=True)  51.9 us
    all_to_all x1, blocking collectives, local(): lax.all_to_all(mixed, 'grp', split_axis=0, concat_axis=0, tiled=True)  14.6 us
    pallas_call x1, Pallas kernels, share_facts(): pl.pallas_call(functools.partial(facts_kernel, groups, tp_count), out_sha...  10.9 us
    dot_general x1, matrix products, local(): jnp.dot(arrived, query_weight[0], preferred_element_type=f32).astype(bf16)  10.3 us
    all_to_all x1, starting transfers between devices, to_owner(): lax.all_to_all(partial, 'grp', split_axis=0, concat_axis=0, tiled=True)  9.18 us
    sub x1, matrix products, local(): powered = jnp.exp(scores - jnp.max(scores, axis=2, keepdims=True))  5.7 us
    dot_general x1, matrix products, local(): jnp.einsum('gsp,gpc->gsc', expand, own_first, preferred_element_type=f32)  5.39 us
  transfers between devices with their start and end apart: 3, of which 3 were waited for; matrix products, arithmetic and copies ran while one was open for 2% of the time, Pallas kernels for 0%

profile of v2, /device:TPU:0, one launch (start us, length us, event | category | flops | bytes accessed | tf_op | source)
XLA Modules:
  0.0 267.3 jit_solution(8758081560201005185)
XLA Ops:
  0.0 0.0 copy-start
  0.0 0.0 copy-start.4
  0.0 0.0 copy-start.6
  0.0 0.0 copy-start.7
  0.0 0.0 copy-start.8
  0.0 2.7 %fusion.3 = f32[768]{0:T(1024)S(1)} fusion(bf16[768,2048]{1,0:T(8,128)(2,1)} %param.7), kind=kLoop, calls=%fused_computation.13 | loop fusion | flops 4717824 | bytes 3148800 | tf_op jit(solution)/shard_map/reduce_sum | solution.py:262
  2.8 0.0 copy-done.6
  2.8 0.0 copy-done.7
  2.8 0.0 copy-done.8
  2.8 0.7 select_select_fusion.facts
  3.5 10.9 %share_facts.1 = (f32[4,8,768]{2,1,0:T(8,128)}, f32[4,8,768]{2,1,0:T(8,128)}) custom-call(f32[8,768]{1,0:T(8,128)} %select_select_fusion.facts), custom_call_target="tpu_custom_call" | custom-call | tf_op jit(solution)/shard_map/share_facts/pallas_call | solution.py:87
  14.4 0.9 slice_convert_fusion
  15.3 1.0 and_select_fusion.1
  16.3 1.0 iota_compare_fusion.6
  17.3 0.9 slice_reduce_fusion
  18.3 0.0 copy-done
  18.3 5.2 %convert_reduce_fusion = (s32[4,768]{1,0:T(4,128)S(1)}, s32[4,768]{1,0:T(4,128)S(1)}) fusion(s32[4,768]{1,0:T(4,128)S(1)} %get-tuple-element.22, s32[4,768]{1,0:T(4,128)S(1)} %bitcast.86, pred[768,768]{1,0:T(8,128)(4,1)} %iota_compare_fusion.6, s32[4,768]{1,0:T(4,128)S(1)} %get-tuple-element.21, s32[4,768]{1,0:T(4,128)S(1)} %bitcast.85), kind=kLoop, calls=%fused_computation.6 | loop fusion | flops 18868224 | bytes 663552 | tf_op jit(solution)/shard_map/reduce_sum | solution.py:275
  23.6 0.0 copy-done.4
  23.6 1.6 fusion.28.chosen
  25.2 109.0 %move_tokens.1 = bf16[4,384,2048]{2,1,0:T(8,128)(2,1)S(1)} custom-call(bf16[384,2048]{1,0:T(8,128)(2,1)S(1)} %fusion.28.chosen), custom_call_target="tpu_custom_call" | custom-call | tf_op jit(solution)/shard_map/move_tokens/pallas_call | solution.py:221
  134.2 0.0 copy-start.2
  134.3 2.7 copy-done.2
  136.9 0.0 copy-start.3
  136.9 10.3 %fusion.16 = bf16[1536,1024]{0,1:T(8,128)(2,1)S(1)} fusion(bf16[1536,2048]{1,0:T(8,128)(2,1)} %bitcast.73, bf16[1,2048,1024]{2,1,0:T(8,128)(2,1)} %param.12), kind=kOutput, calls=%fused_computation.26 | convolution fusion | flops 6444023808 | bytes 13631488 | tf_op jit(solution)/shard_map/dot_general | solution.py:292
  147.2 0.0 copy-done.3
  147.2 3.1 %convolution_convert_fusion = bf16[1536,256]{0,1:T(8,128)(2,1)S(1)} fusion(bf16[1536,2048]{1,0:T(8,128)(2,1)S(1)} %bitcast.74, bf16[1,2048,1024]{2,1,0:T(8,128)(2,1)} %param.13, s32[]{:T(128)S(6)} %select_n.143), kind=kOutput, calls=%fused_computation.37 | convolution fusion | flops 1611005952 | bytes 8126468 | tf_op jit(solution)/shard_map/dot_general | solution.py:293
  150.3 0.2 constant_dynamic-slice_fusion.1
  150.5 1.8 pad_maximum_fusion.1
  152.3 0.0 collective-permute-start
  152.4 2.5 copy.57
  154.8 0.0 copy-start.5
  154.8 1.2 select_reduce_fusion
  156.0 1.1 collective-permute-done
  157.2 4.3 %copy.58 = bf16[1536,768]{1,0:T(8,128)(2,1)} copy(bf16[1536,768]{0,1:T(8,128)(2,1)} %collective-permute-done) | data formatting | bytes 4718592 | tf_op jit(solution)/shard_map/reshape | solution.py:300
  161.4 0.0 copy-done.5
  161.4 5.4 %fusion.25 = bf16[4,768,768]{2,1,0:T(8,128)(2,1)S(1)} fusion(bf16[4,384,768]{2,1,0:T(8,128)(2,1)} %bitcast.79, bf16[4,384,768]{2,1,0:T(8,128)(2,1)S(1)} %bitcast.78, s32[4,768]{1,0:T(4,128)S(1)} %compare_select_fusion.4), kind=kOutput, calls=%fused_computation.33 | convolution fusion | flops 3638034432 | bytes 9449472 | tf_op jit(solution)/shard_map/gsp,gpc->gsc/dot_general | solution.py:305
  166.8 2.6 copy.48
  169.4 9.2 %all-to-all-start = ((bf16[4,768,768]{2,1,0:T(8,128)(2,1)}), bf16[4,768,768]{2,1,0:T(8,128)(2,1)}, u32[]{:S(2)}, u32[]{:S(2)}) async-start(bf16[4,768,768]{2,1,0:T(8,128)(2,1)} %bitcast.75), calls=%async_computation | async-start | bytes 9437184 | tf_op jit(solution)/shard_map/all_to_all | solution.py:242
  178.6 0.7 fusion.31
  179.3 0.1 reshape.340
  179.4 0.1 broadcast_add_fusion
  179.4 0.1 add.176
  179.6 1.0 or_and_fusion
  180.5 51.9 %all-to-all-done = bf16[4,768,768]{2,1,0:T(8,128)(2,1)} async-done(((bf16[4,768,768]{2,1,0:T(8,128)(2,1)}), bf16[4,768,768]{2,1,0:T(8,128)(2,1)}, u32[]{:S(2)}, u32[]{:S(2)}) %all-to-all-start) | async-done | bytes 4718624 | tf_op jit(solution)/shard_map/all_to_all | solution.py:242
  232.5 3.8 %reduce_sum.95 = bf16[768,768]{1,0:T(8,128)(2,1)S(1)} reduce(bf16[4,768,768]{2,1,0:T(8,128)(2,1)} %all-to-all-done, bf16[]{:T(256)} %constant.136.clone.1), dimensions={0}, to_apply=%region_5.6 | reduce | flops 1769472 | bytes 5898242 | tf_op jit(solution)/shard_map/reduce_sum | solution.py:308
  236.2 0.1 slice.22
  236.3 0.3 copy.49
  236.6 5.7 %fusion.70 = (f32[4,768]{1,0:T(4,128)S(1)}, f32[4,768,768]{1,2,0:T(8,128)}) fusion(pred[768,768]{0,1:T(8,128)(4,1)S(1)} %or_and_fusion, bf16[768,4,128]{0,2,1:T(8,128)(2,1)S(1)} %bitcast.80, bf16[768,768]{1,0:T(8,128)(2,1)S(1)} %reduce_sum.95), kind=kOutput, calls=%fused_computation.129 | convolution fusion | flops 613417728 | bytes 11022336 | tf_op jit(solution)/shard_map/sub | solution.py:328
  242.3 4.5 %fusion.48 = bf16[768,4,128]{0,2,1:T(8,128)(2,1)S(1)} fusion(f32[4,768,768]{1,2,0:T(8,128)} %get-tuple-element.24, f32[4,768]{1,0:T(4,128)S(1)} %get-tuple-element.23, bf16[768,768]{1,0:T(8,128)(2,1)S(1)} %reduce_sum.95), kind=kOutput, calls=%fused_computation.51 | convolution fusion | flops 609091584 | bytes 10432512 | tf_op jit(solution)/shard_map/hqk,kd->qhd/dot_general | solution.py:330
  246.8 0.6 copy.53
  247.4 0.3 all_to_all.12
  247.7 14.6 %all_to_all.17 = bf16[4,192,512]{2,1,0:T(8,128)(2,1)S(1)} all-to-all(bf16[4,192,512]{2,1,0:T(8,128)(2,1)S(1)} %all_to_all.12), channel_id=1, replica_groups=mesh['tower'=2,'tp'=4,'grp'=4] {'grp'}, dimensions={0} | all-to-all | bytes 1572864 | tf_op jit(solution)/shard_map/all_to_all | solution.py:333
  262.2 0.0 collective-permute-start.1
  262.3 2.2 collective-permute-done.1
  264.5 0.2 broadcast_select_fusion.1
  264.7 0.0 copy-start.1
  264.7 2.6 fusion.42
  267.3 0.0 copy-done.1
  (22 shorter events, 0.3 us)
Async XLA Ops:
  0.0 18.3 %copy-start = (f32[1,8192]{1,0:T(1,128)S(1)}, f32[1,8192]{1,0:T(1,128)}, u32[]{:S(2)}) copy-start(f32[1,8192]{1,0:T(1,128)} %param.11) | copy-start | bytes 98308
  0.0 23.6 %copy-start.4 = (bf16[768,2048]{1,0:T(8,128)(2,1)S(1)}, bf16[768,2048]{1,0:T(8,128)(2,1)}, u32[]{:S(2)}) copy-start(bf16[768,2048]{1,0:T(8,128)(2,1)} %param.7) | copy-start | bytes 9437188
  0.0 2.8 %copy-start.6 = (s32[768]{0:T(1024)S(1)}, s32[768]{0:T(1024)}, u32[]{:S(2)}) copy-start(s32[768]{0:T(1024)} %param.8) | copy-start | bytes 9220
  0.0 2.8 %copy-start.7 = (s32[768]{0:T(1024)S(1)}, s32[768]{0:T(1024)}, u32[]{:S(2)}) copy-start(s32[768]{0:T(1024)} %param.10) | copy-start | bytes 9220
  0.0 2.8 %copy-start.8 = (s32[768]{0:T(1024)S(1)}, s32[768]{0:T(1024)}, u32[]{:S(2)}) copy-start(s32[768]{0:T(1024)} %param.9) | copy-start | bytes 9220
  134.2 2.7 copy-start.2
  136.9 10.3 %copy-start.3 = (bf16[4,384,2048]{2,1,0:T(8,128)(2,1)S(1)}, bf16[4,384,2048]{2,1,0:T(8,128)(2,1)}, u32[]{:S(2)}) copy-start(bf16[4,384,2048]{2,1,0:T(8,128)(2,1)} %copy-done.2) | copy-start | bytes 18874372
  152.3 4.9 %collective-permute-start = (bf16[1536,768]{0,1:T(8,128)(2,1)}, bf16[1536,768]{0,1:T(8,128)(2,1)}, u32[]{:S(2)}, u32[]{:S(2)}) collective-permute-start(bf16[1536,768]{0,1:T(8,128)(2,1)} %get-tuple-element.20), channel_id=1, source_target_pairs={{0,16},{16,0},{1,17},{17,1},{2,18},{18,2},{3,19},{19,3},{4,20},{20... | collective-permute-start | bytes 7077896 | tf_op jit(solution)/shard_map/ppermute | solution.py:17
  154.8 6.6 %copy-start.5 = (bf16[1536,768]{1,0:T(8,128)(2,1)S(1)}, bf16[1536,768]{1,0:T(8,128)(2,1)}, u32[]{:S(2)}) copy-start(bf16[1536,768]{1,0:T(8,128)(2,1)} %copy.57) | copy-start | bytes 7077892
  169.4 63.0 %all-to-all-start = ((bf16[4,768,768]{2,1,0:T(8,128)(2,1)}), bf16[4,768,768]{2,1,0:T(8,128)(2,1)}, u32[]{:S(2)}, u32[]{:S(2)}) async-start(bf16[4,768,768]{2,1,0:T(8,128)(2,1)} %bitcast.75), calls=%async_computation | async-start | bytes 9437184 | tf_op jit(solution)/shard_map/all_to_all | solution.py:242
  262.2 2.3 collective-permute-start.1
  264.7 2.6 copy-start.1

commit v3 on v2

--- a/solution.py
+++ b/solution.py
@@ -285,27 +285,46 @@
     normed = (values * inverse_rms[:, None] * gain[None, :]).astype(bf16)
     choose = packed_here[None, :] == (tower * half + jnp.arange(half, dtype=i32))[:, None]
     chosen = pick(choose, normed)
-    arrived = move_tokens(chosen, groups, tp_count).reshape(groups * half, width)
-
-    pair_part = lax.dynamic_slice_in_dim(pair_weight[0], own_head * 2 * HD, 2 * HD, 1)
+    arrived = move_tokens(chosen, groups, tp_count)
+
+    pair_cut = lax.dynamic_slice_in_dim(pair_weight[0], own_head * 2 * HD, 2 * HD, 1)
     half_cols = head_cols // 2
-    query_part = jnp.dot(arrived, query_weight[0], preferred_element_type=f32).astype(bf16)
-    pair_part = jnp.dot(arrived, pair_part, preferred_element_type=f32).astype(bf16)
-    query_keep = lax.dynamic_slice_in_dim(query_part, tower * half_cols, half_cols, 1)
-    query_give = lax.dynamic_slice_in_dim(query_part, (1 - tower) * half_cols, half_cols, 1)
-    keep = jnp.concatenate([query_keep, pair_part], axis=1)
-    got = swap_tower(jnp.concatenate([query_give, pair_part], axis=1))
-    cols = half_cols + 2 * HD
-    keep = keep.reshape(groups, half, cols)
-    got = got.reshape(groups, half, cols)
-    own_first = jnp.concatenate([keep, got], axis=1)
+    cols = half_cols + HD
     position = packed_of_slot - tower * half
     position = jnp.where(position < 0, position + tok, position)
-    expand = (position[:, :, None] == where_i[None, None, :]).astype(bf16)
-    slotted = jnp.einsum("gsp,gpc->gsc", expand, own_first, preferred_element_type=f32).astype(bf16)
-    by_owner = slotted.reshape(groups, groups, slot_count, cols).transpose(1, 0, 2, 3)
-    parts = to_owner(by_owner.reshape(groups, tok, cols))
-    rows = jnp.sum(parts.astype(f32), axis=0).astype(bf16)
+    pieces = 2
+    step = groups // pieces
+    summed = []
+    for piece in range(pieces):
+        these = arrived[piece * step : (piece + 1) * step].reshape(step * half, width)
+        query_part = jnp.dot(these, query_weight[0], preferred_element_type=f32).astype(bf16)
+        pair_part = jnp.dot(these, pair_cut, preferred_element_type=f32).astype(bf16)
+
+        def columns(core):
+            return jnp.concatenate(
+                [
+                    lax.dynamic_slice_in_dim(query_part, core * half_cols, half_cols, 1),
+                    lax.dynamic_slice_in_dim(pair_part, core * HD, HD, 1),
+                ],
+                axis=1,
+            )
+
+        got = swap_tower(columns(1 - tower))
+        kept = columns(tower)
+        slotted = []
+        for k in range(step):
+            onehot = (position[piece * step + k][:, None] == where_i[None, :]).astype(bf16)
+            span = slice(k * half, (k + 1) * half)
+            both = jnp.dot(onehot[:, :half], kept[span], preferred_element_type=f32)
+            both += jnp.dot(onehot[:, half:], got[span], preferred_element_type=f32)
+            slotted.append(both.astype(bf16).reshape(groups, slot_count, cols))
+        parts = to_owner(jnp.concatenate(slotted, axis=1))
+        summed.append(jnp.sum(parts.astype(f32), axis=0).astype(bf16))
+    rows = jnp.concatenate(summed, axis=0)
+    own_side = rows[:, half_cols:]
+    far_side = swap_tower(own_side)
+    keys = jnp.where(tower == 0, own_side, far_side)
+    vals = jnp.where(tower == 0, far_side, own_side)
 
     mine = group * slot_count + jnp.arange(slot_count, dtype=i32)
     at_mine = slots[:, None, :] == mine[None, :, None]
@@ -319,8 +338,6 @@
     )
     heads = half_cols // HD
     queries = rows[:, :half_cols].reshape(tok, heads, HD)
-    keys = rows[:, half_cols : half_cols + HD]
-    vals = rows[:, half_cols + HD :]
     scores = jnp.einsum("qhd,kd->hqk", queries, keys, preferred_element_type=f32) * (
         1.0 / math.sqrt(HD)
     )

time: 268 us -> 263 us (0.981)
  waiting for transfers between devices: 55.3 us -> 39.5 us
  matrix products: 33.1 us -> 41.9 us
  local copies, waits for them, and re-layouts: 13.6 us -> 7.49 us
  starting transfers between devices: 9.18 us -> 14.3 us
  other arithmetic: 21.3 us -> 24.1 us
    all_to_all x1 -> x2, waiting for transfers between devices: 51.9 us -> 37.1 us  [to_owner(): lax.all_to_all(partial, 'grp', split_axis=0, concat_axis=0, tiled=True)]
    reshape x3 -> x0, local copies, waits for them, and re-layouts: 9.32 us -> none  [the longest x1 4.28 us: local(): got = got.reshape(groups, half, cols)]
    dot_general x3 -> x12, matrix products: 18.8 us -> 26.1 us  [the longest x2 11.3 us: local(): jnp.dot(these, query_weight[0], preferred_element_type=f32).astype(bf16)]
    all_to_all x1 -> x2, starting transfers between devices: 9.18 us -> 13.6 us  [to_owner(): lax.all_to_all(partial, 'grp', split_axis=0, concat_axis=0, tiled=True)]
    dynamic_slice x1 -> x4, local copies, waits for them, and re-layouts: 0.21 us -> 3.42 us  [the longest x2 1.77 us: columns(): lax.dynamic_slice_in_dim(pair_part, core * HD, HD, 1)]
  transfers between devices with their start and end apart: 3 -> 6, of which waited for: 3 -> 4; matrix products, arithmetic and copies ran while one was open for 2% -> 9% of each run, Pallas kernels for 0% -> 0%
where the time goes in v3:
time: 263 us
  Pallas kernels  120 us (46%)
  matrix products  41.9 us (16%)
  waiting for transfers between devices  39.5 us (15%)
  other arithmetic  24.1 us (9%)
  blocking collectives  14.9 us (6%)
  starting transfers between devices  14.3 us (5%)
  local copies, waits for them, and re-layouts  7.49 us (3%)
    pallas_call x1, Pallas kernels, move_tokens(): pl.pallas_call(functools.partial(tokens_kernel, groups, tp_count, chunks)...  109 us
    all_to_all x2, waiting for transfers between devices, to_owner(): lax.all_to_all(partial, 'grp', split_axis=0, concat_axis=0, tiled=True)  37.1 us
    all_to_all x1, blocking collectives, local(): lax.all_to_all(mixed, 'grp', split_axis=0, concat_axis=0, tiled=True)  14.9 us
    all_to_all x2, starting transfers between devices, to_owner(): lax.all_to_all(partial, 'grp', split_axis=0, concat_axis=0, tiled=True)  13.6 us
    dot_general x2, matrix products, local(): jnp.dot(these, query_weight[0], preferred_element_type=f32).astype(bf16)  11.3 us
    pallas_call x1, Pallas kernels, share_facts(): pl.pallas_call(functools.partial(facts_kernel, groups, tp_count), out_sha...  10.9 us
    sub x1, matrix products, local(): powered = jnp.exp(scores - jnp.max(scores, axis=2, keepdims=True))  6.99 us
    dot_general x4, matrix products, local(): both += jnp.dot(onehot[:, half:], got[span], preferred_element_type=f32)  5.53 us
  transfers between devices with their start and end apart: 6, of which 4 were waited for; matrix products, arithmetic and copies ran while one was open for 9% of the time, Pallas kernels for 0%

profile of v3, /device:TPU:0, one launch (start us, length us, event | category | flops | bytes accessed | tf_op | source)
XLA Modules:
  0.0 262.6 jit_solution(5995156434488861590)
XLA Ops:
  0.0 2.7 %fusion.2 = f32[768]{0:T(1024)S(1)} fusion(bf16[768,2048]{1,0:T(8,128)(2,1)} %param.7), kind=kLoop, calls=%fused_computation.11 | loop fusion | flops 4717824 | bytes 3148800 | tf_op jit(solution)/shard_map/reduce_sum | solution.py:262
  2.8 0.7 select_select_fusion.facts
  3.5 10.9 %share_facts.1 = (f32[4,8,768]{2,1,0:T(8,128)}, f32[4,8,768]{2,1,0:T(8,128)}) custom-call(f32[8,768]{1,0:T(8,128)} %select_select_fusion.facts), custom_call_target="tpu_custom_call" | custom-call | tf_op jit(solution)/shard_map/share_facts/pallas_call | solution.py:87
  14.4 0.9 slice_convert_fusion
  15.3 1.0 and_select_fusion.1
  16.3 1.0 iota_compare_fusion.6
  17.4 5.2 %convert_reduce_fusion = (s32[4,768]{1,0:T(4,128)S(1)}, s32[4,768]{1,0:T(4,128)S(1)}) fusion(s32[4,768]{1,0:T(4,128)S(1)} %get-tuple-element.32, s32[4,768]{1,0:T(4,128)S(1)} %bitcast.95, pred[768,768]{1,0:T(8,128)(4,1)} %iota_compare_fusion.6, s32[4,768]{1,0:T(4,128)S(1)} %get-tuple-element.31, s32[4,768]{1,0:T(4,128)S(1)} %bitcast.96), kind=kLoop, calls=%fused_computation.5 | loop fusion | flops 18868224 | bytes 663552 | tf_op jit(solution)/shard_map/reduce_sum | solution.py:275
  22.7 1.2 select_reduce_fusion
  23.9 0.9 slice_reduce_fusion
  24.9 0.1 slice_reduce_fusion.4
  25.0 1.6 fusion.19.chosen
  26.6 109.0 %move_tokens.1 = bf16[4,384,2048]{2,1,0:T(8,128)(2,1)S(1)} custom-call(bf16[384,2048]{1,0:T(8,128)(2,1)S(1)} %fusion.19.chosen), custom_call_target="tpu_custom_call" | custom-call | tf_op jit(solution)/shard_map/move_tokens/pallas_call | solution.py:221
  135.6 2.5 fusion.108
  138.1 7.8 %fusion.30 = bf16[768,1024]{1,0:T(8,128)(2,1)} fusion(bf16[768,2048]{1,0:T(8,128)(2,1)} %bitcast.87, bf16[1,2048,1024]{2,1,0:T(8,128)(2,1)} %param.12), kind=kOutput, calls=%fused_computation.47 | convolution fusion | flops 3222011904 | bytes 8912896 | tf_op jit(solution)/shard_map/dot_general | solution.py:300
  146.0 2.9 %convolution_convert_fusion.1 = bf16[768,256]{1,0:T(8,128)(2,1)} fusion(bf16[768,2048]{1,0:T(8,128)(2,1)S(1)} %bitcast.88, bf16[1,2048,1024]{2,1,0:T(8,128)(2,1)} %param.13, s32[]{:T(128)S(6)} %select_n.162), kind=kOutput, calls=%fused_computation.56 | convolution fusion | flops 805502976 | bytes 4587524 | tf_op jit(solution)/shard_map/dot_general | solution.py:301
  148.9 1.0 constant_dynamic-slice_fusion.5
  150.0 1.5 constant_dynamic-slice_fusion.6
  151.4 0.1 pad_maximum_fusion.2
  151.5 0.1 collective-permute-start
  151.6 2.4 convolution_convert_fusion
  154.0 0.1 copy-done.8
  154.1 3.5 %fusion.33 = bf16[768,1024]{1,0:T(8,128)(2,1)S(1)} fusion(bf16[768,2048]{1,0:T(8,128)(2,1)S(1)} %bitcast.86, bf16[1,2048,1024]{2,1,0:T(8,128)(2,1)S(1)} %copy-done.8), kind=kOutput, calls=%fused_computation.48 | convolution fusion | flops 3222011904 | bytes 8912896 | tf_op jit(solution)/shard_map/dot_general | solution.py:300
  157.6 0.7 constant_dynamic-slice_fusion.1
  158.3 0.2 constant_dynamic-slice_fusion.2
  158.5 1.0 pad_maximum_fusion.3
  159.6 0.5 collective-permute-start.1
  160.0 0.4 iota_compare_fusion.4
  160.4 0.4 iota_compare_fusion.3
  160.8 0.4 iota_compare_fusion.2
  161.3 0.7 fusion.58
  162.0 0.7 fusion.55
  162.8 0.8 add_convert_fusion.3
  163.6 1.0 add_convert_fusion.2
  164.6 1.5 pad_maximum_fusion
  166.0 9.2 %all-to-all-start = ((bf16[4,384,640]{2,1,0:T(8,128)(2,1)}), bf16[4,384,640]{2,1,0:T(8,128)(2,1)S(1)}, u32[]{:S(2)}, u32[]{:S(2)}) async-start(bf16[4,384,640]{2,1,0:T(8,128)(2,1)} %pad_maximum_fusion), calls=%async_computation | async-start | bytes 3932160 | tf_op jit(solution)/shard_map/all_to_all | solution.py:242
  175.2 0.4 iota_compare_fusion.1
  175.6 1.7 fusion.52
  177.3 0.7 fusion.49
  178.1 1.9 add_convert_fusion.1
  180.0 1.9 add_convert_fusion
  181.8 1.5 pad_maximum_fusion.1
  183.3 15.6 %all-to-all-done = bf16[4,384,640]{2,1,0:T(8,128)(2,1)S(1)} async-done(((bf16[4,384,640]{2,1,0:T(8,128)(2,1)}), bf16[4,384,640]{2,1,0:T(8,128)(2,1)S(1)}, u32[]{:S(2)}, u32[]{:S(2)}) %all-to-all-start) | async-done | bytes 1966112 | tf_op jit(solution)/shard_map/all_to_all | solution.py:242
  198.9 4.4 %all-to-all-start.1 = ((bf16[4,384,640]{2,1,0:T(8,128)(2,1)}), bf16[4,384,640]{2,1,0:T(8,128)(2,1)}, u32[]{:S(2)}, u32[]{:S(2)}) async-start(bf16[4,384,640]{2,1,0:T(8,128)(2,1)} %pad_maximum_fusion.1), calls=%async_computation.1 | async-start | bytes 3932160 | tf_op jit(solution)/shard_map/all_to_all | solution.py:242
  203.3 0.7 fusion.22
  204.0 0.1 reshape.342
  204.1 0.1 broadcast_add_fusion
  204.2 0.1 add.200
  204.3 0.6 reduce_sum.107
  204.8 21.5 %all-to-all-done.1 = bf16[4,384,640]{2,1,0:T(8,128)(2,1)} async-done(((bf16[4,384,640]{2,1,0:T(8,128)(2,1)}), bf16[4,384,640]{2,1,0:T(8,128)(2,1)}, u32[]{:S(2)}, u32[]{:S(2)}) %all-to-all-start.1) | async-done | bytes 1966112 | tf_op jit(solution)/shard_map/all_to_all | solution.py:242
  226.3 2.1 reduce_sum.108
  228.4 0.1 collective-permute-start.2
  228.5 1.0 or_and_fusion
  229.5 0.1 pad_maximum_fusion.4
  229.6 0.3 copy.66
  229.8 0.2 collective-permute-done.2
  230.1 7.0 %fusion.109 = (f32[4,768]{1,0:T(4,128)S(1)}, f32[4,768,768]{1,2,0:T(8,128)}) fusion(pred[768,768]{0,1:T(8,128)(4,1)S(1)} %or_and_fusion, bf16[768,4,128]{0,2,1:T(8,128)(2,1)S(1)} %bitcast.90, bf16[768,128]{1,0:T(8,128)(2,1)S(1)} %pad_maximum_fusion.9, bf16[768,128]{1,0:T(8,128)(2,1)} %collective-permute-done.2, pred[]{:T(512)S(6)} %eq.211), kind=kOutput, calls=%fused_computation.189 | convolution fusion | flops 613516032 | bytes 11218945 | tf_op jit(solution)/shard_map/sub | solution.py:345
  237.1 4.6 %fusion.45 = bf16[768,4,128]{0,2,1:T(8,128)(2,1)S(1)} fusion(f32[4,768,768]{1,2,0:T(8,128)} %get-tuple-element.34, f32[4,768]{1,0:T(4,128)S(1)} %get-tuple-element.33, bf16[768,128]{1,0:T(8,128)(2,1)} %collective-permute-done.2, bf16[768,128]{1,0:T(8,128)(2,1)S(1)} %pad_maximum_fusion.9, pred[]{:T(512)S(6)} %eq.211), kind=kOutput, calls=%fused_computation.54 | convolution fusion | flops 609189888 | bytes 10629121 | tf_op jit(solution)/shard_map/hqk,kd->qhd/dot_general | solution.py:347
  241.7 0.6 copy.70
  242.3 0.3 all_to_all.16
  242.6 14.9 %all_to_all.22 = bf16[4,192,512]{2,1,0:T(8,128)(2,1)S(1)} all-to-all(bf16[4,192,512]{2,1,0:T(8,128)(2,1)S(1)} %all_to_all.16), channel_id=1, replica_groups=mesh['tower'=2,'tp'=4,'grp'=4] {'grp'}, dimensions={0} | all-to-all | bytes 1572864 | tf_op jit(solution)/shard_map/all_to_all | solution.py:350
  257.6 0.1 collective-permute-start.3
  257.7 2.2 collective-permute-done.3
  259.8 0.2 broadcast_select_fusion.1
  260.0 2.6 fusion.39
  (42 shorter events, 0.3 us)
Async XLA Ops:
  0.0 24.9 %copy-start = (f32[1,8192]{1,0:T(1,128)S(1)}, f32[1,8192]{1,0:T(1,128)}, u32[]{:S(2)}) copy-start(f32[1,8192]{1,0:T(1,128)} %param.11) | copy-start | bytes 98308
  0.0 2.8 %copy-start.6 = (s32[768]{0:T(1024)S(1)}, s32[768]{0:T(1024)}, u32[]{:S(2)}) copy-start(s32[768]{0:T(1024)} %param.10) | copy-start | bytes 9220
  0.0 2.8 %copy-start.5 = (s32[768]{0:T(1024)S(1)}, s32[768]{0:T(1024)}, u32[]{:S(2)}) copy-start(s32[768]{0:T(1024)} %param.8) | copy-start | bytes 9220
  0.0 2.8 %copy-start.7 = (s32[768]{0:T(1024)S(1)}, s32[768]{0:T(1024)}, u32[]{:S(2)}) copy-start(s32[768]{0:T(1024)} %param.9) | copy-start | bytes 9220
  0.0 24.9 %copy-start.2 = (bf16[768,2048]{1,0:T(8,128)(2,1)S(1)}, bf16[768,2048]{1,0:T(8,128)(2,1)}, u32[]{:S(2)}) copy-start(bf16[768,2048]{1,0:T(8,128)(2,1)} %param.7) | copy-start | bytes 9437188
  138.1 7.8 %copy-start.3 = (bf16[2,384,2048]{2,1,0:T(8,128)(2,1)S(1)}, bf16[2,384,2048]{2,1,0:T(8,128)(2,1)}, u32[]{:S(2)}) copy-start(bf16[2,384,2048]{2,1,0:T(8,128)(2,1)} %get-tuple-element.19) | copy-start | bytes 9437188
  151.5 11.2 %collective-permute-start = (bf16[768,640]{1,0:T(8,128)(2,1)S(1)}, bf16[768,640]{1,0:T(8,128)(2,1)S(1)}, u32[]{:S(2)}, u32[]{:S(2)}) collective-permute-start(bf16[768,640]{1,0:T(8,128)(2,1)S(1)} %pad_maximum_fusion.2), channel_id=1, source_target_pairs={{0,16},{16,0},{1,17},{17,1},{2,18},{18,2},{3,19},{19,3},{4,20},{20... | collective-permute-start | bytes 2949128 | tf_op jit(solution)/shard_map/ppermute | solution.py:17
  151.6 2.5 copy-start.8
  159.6 18.5 %collective-permute-start.1 = (bf16[768,640]{1,0:T(8,128)(2,1)}, bf16[768,640]{1,0:T(8,128)(2,1)}, u32[]{:S(2)}, u32[]{:S(2)}) collective-permute-start(bf16[768,640]{1,0:T(8,128)(2,1)} %pad_maximum_fusion.3), channel_id=1, source_target_pairs={{0,16},{16,0},{1,17},{17,1},{2,18},{18,2},{3,19},{19,3},{4,20},{20... | collective-permute-start | bytes 2949128 | tf_op jit(solution)/shard_map/ppermute | solution.py:17
  166.0 32.8 %all-to-all-start = ((bf16[4,384,640]{2,1,0:T(8,128)(2,1)}), bf16[4,384,640]{2,1,0:T(8,128)(2,1)S(1)}, u32[]{:S(2)}, u32[]{:S(2)}) async-start(bf16[4,384,640]{2,1,0:T(8,128)(2,1)} %pad_maximum_fusion), calls=%async_computation | async-start | bytes 3932160 | tf_op jit(solution)/shard_map/all_to_all | solution.py:242
  175.2 2.1 copy-start.4
  198.9 27.5 %all-to-all-start.1 = ((bf16[4,384,640]{2,1,0:T(8,128)(2,1)}), bf16[4,384,640]{2,1,0:T(8,128)(2,1)}, u32[]{:S(2)}, u32[]{:S(2)}) async-start(bf16[4,384,640]{2,1,0:T(8,128)(2,1)} %pad_maximum_fusion.1), calls=%async_computation.1 | async-start | bytes 3932160 | tf_op jit(solution)/shard_map/all_to_all | solution.py:242
  228.4 1.6 collective-permute-start.2
  257.6 2.3 collective-permute-start.3
  260.0 2.6 copy-start.1
